TPU v7x, 32 devices: a whole 2x2x4 slice. The times are simulated.
32 devices in a mesh: dp: 4 (over x, core), vocab: 8 (over z, y).
Axes of the slice: x: 2, y: 2, z: 4, core: 2. Of those that a mesh axis runs over, the one named last changes fastest.
Arguments:
- hidden: bfloat16 [256, 3584], P('dp'), may hold values from -160 to 160
- head_weight: bfloat16 [3584, 152064], P(None, ('dp', 'vocab')), may hold values from -0.3125 to 0.3125
- teacher_ids: int32 [256, 64], P('dp'), may hold values from 0 to 152063, as said below
- teacher_probs: float32 [256, 64], P('dp'), may hold values from 0 to 0.99, as said below
- token_weight: float32 [256], P('dp'), may hold values from 4 to 32
Outputs:
- divergence: float32 [256], P('dp')
- hidden_grad: float32 [256, 3584], P('dp', 'vocab')
Inputs may be any that keep to these rules, and one draw needn't show every extreme that they name: `teacher_ids`: each row names 64 different vocabulary entries. `teacher_probs`: all positive; each row sums to between 0.5 and 0.99.
All inputs are finite; a program needn't handle non-finite values.
Results may differ from a plain program's by a relative error of at most 0.0029.
Values may be sent and summed in bfloat16 or wider, within the bound.
A program may use at most 128 MiB of HBM per device.

v0:
```python
import functools

import jax
import jax.numpy as jnp
from jax import lax
from jax.experimental import pallas as pl
from jax.experimental.pallas import tpu as pltpu
from jax.sharding import PartitionSpec as P

MESH = pl.DeviceIdType.MESH
NT = (((1,), (1,)), ((), ()))


def windows(feat):
    q = next(k for k in (1, 2, 4, 8, 16, 32, 64, 128) if k * feat % 128 == 0)
    first = [m * feat // 128 * 128 for m in range(q)]
    ww = max((m + 1) * feat - first[m] + 127 for m in range(q)) // 128 * 128
    return q, ww, [min(f, q * feat - ww) for f in first]


def kernel(
    ndp, nv, kc, hid, w, ids_in, probs_in, tw, div_out, grad_out,
    wv, h_all, tp_all, sp, logits, lg, g, r1, sx, rx, s2, r2, stats, cols, cols2, back, own,
    w_sem, l_sem, hx_s, hx_r, hc_s, hc_r, tp_s, tp_r, st_s, st_r, g1_s, g1_r, gx_s, gx_r, g2_s, g2_r,
):
    d, mv = lax.axis_index("dp"), lax.axis_index("vocab")
    x, core = d // 2, d % 2
    nx, nd = ndp // 2, ndp * nv
    me = d * nv + mv
    rows, depth = hid.shape
    cols_n = w.shape[0]
    tok = rows * ndp
    nk = depth // kc
    nt = (cols_n + 127) // 128
    feat = depth // nv
    q, ww, starts = windows(feat)
    ng, group = nv // q, q * feat
    mg, mm = mv // q, lax.rem(mv, q)
    other = (2 * x + 1 - core, mv)

    def block(dp_index):
        return pl.ds(pl.multiple_of(dp_index * rows, rows), rows)

    def w_copy(c):
        part = pl.ds(pl.multiple_of(c * kc, kc), kc)
        return pltpu.make_async_copy(w.at[:, part], wv.at[:, part], w_sem.at[c])

    def l_copy():
        return pltpu.make_async_copy(hid, h_all.at[block(d), :], l_sem.at[0])

    def kpart(c):
        return pl.ds(pl.multiple_of(c * kc, kc), kc)

    def hx_copy(j, c):
        return pltpu.make_async_remote_copy(
            src_ref=hid.at[:, kpart(c)], dst_ref=h_all.at[block(d), kpart(c)],
            send_sem=hx_s.at[j - 1, c], recv_sem=hx_r.at[j - 1, c],
            device_id=(2 * lax.rem(x + j, nx) + core, mv), device_id_type=MESH)

    def hx_in(j, c):
        src = block(2 * lax.rem(x + nx - j, nx) + core)
        return pltpu.make_async_remote_copy(
            src_ref=h_all.at[src, kpart(c)], dst_ref=h_all.at[src, kpart(c)],
            send_sem=hx_s.at[j - 1, c], recv_sem=hx_r.at[j - 1, c],
            device_id=other, device_id_type=MESH)

    def hc_copy(j, c):
        if j == 0:
            src = hid.at[:, kpart(c)]
        else:
            src = h_all.at[block(2 * lax.rem(x + nx - j, nx) + core), kpart(c)]
        return pltpu.make_async_remote_copy(
            src_ref=src,
            dst_ref=h_all.at[block(2 * lax.rem(x + nx - j, nx) + core), kpart(c)],
            send_sem=hc_s.at[j, c], recv_sem=hc_r.at[j, c],
            device_id=other, device_id_type=MESH)

    def hc_in(j, c):
        dst = h_all.at[block(2 * lax.rem(x + nx - j, nx) + 1 - core), kpart(c)]
        return pltpu.make_async_remote_copy(
            src_ref=dst, dst_ref=dst, send_sem=hc_s.at[j, c], recv_sem=hc_r.at[j, c],
            device_id=other, device_id_type=MESH)

    def tp_copy(j, sender):
        return pltpu.make_async_remote_copy(
            src_ref=tp_all.at[block(sender), :],
            dst_ref=tp_all.at[block(sender), :],
            send_sem=tp_s.at[j - 1], recv_sem=tp_r.at[j - 1],
            device_id=(lax.rem(d + j, ndp), mv), device_id_type=MESH)

    def st_copy(j, sender):
        to = lax.rem(me + j, nd)
        return pltpu.make_async_remote_copy(
            src_ref=stats.at[sender], dst_ref=stats.at[sender],
            send_sem=st_s.at[j - 1], recv_sem=st_r.at[j - 1],
            device_id=(to // nv, lax.rem(to, nv)), device_id_type=MESH)

    def g1_copy(i, jx):
        theirs = block(2 * lax.rem(x + jx, nx) + 1 - core)
        return pltpu.make_async_remote_copy(
            src_ref=g.at[i, theirs, :], dst_ref=r1.at[i, jx],
            send_sem=g1_s.at[i, jx], recv_sem=g1_r.at[i, jx],
            device_id=other, device_id_type=MESH)

    def gx_copy(i, jx):
        return pltpu.make_async_remote_copy(
            src_ref=sx.at[i, jx - 1], dst_ref=rx.at[i, jx - 1],
            send_sem=gx_s.at[i, jx - 1], recv_sem=gx_r.at[i, jx - 1],
            device_id=(2 * lax.rem(x + jx, nx) + core, mv), device_id_type=MESH)

    def g2_copy(i, m):
        return pltpu.make_async_remote_copy(
            src_ref=s2.at[i, m], dst_ref=r2.at[i, mm],
            send_sem=g2_s.at[i, m], recv_sem=g2_r.at[i, mm],
            device_id=(d, lax.rem(mg + 1 + i, ng) * q + m), device_id_type=MESH)

    def g2_in(i, m):
        return pltpu.make_async_remote_copy(
            src_ref=r2.at[i, m], dst_ref=r2.at[i, m],
            send_sem=g2_s.at[i, m], recv_sem=g2_r.at[i, m],
            device_id=other, device_id_type=MESH)

    for c in range(nk):
        w_copy(c).start()
    l_copy().start()

    top_n = ids_in.shape[1]
    tp_all[block(d), 0:top_n] = ids_in[...].astype(jnp.float32)
    tp_all[block(d), top_n:2 * top_n] = probs_in[...]

    barrier = pltpu.get_barrier_semaphore()

    def greet(j, _):
        to = lax.rem(me + j, nd)
        pl.semaphore_signal(
            barrier, inc=1, device_id=(to // nv, lax.rem(to, nv)), device_id_type=MESH)
        return 0

    lax.fori_loop(1, nd, greet, 0)
    pl.semaphore_wait(barrier, nd - 1)

    for j in range(1, ndp):
        tp_copy(j, d).start()
    for c in range(nk):
        for j in range(1, nx):
            hx_copy(j, c).start()
        hc_copy(0, c).start()

    for a in range(nt):
        logits[:, a * 128:(a + 1) * 128] = jnp.zeros((tok, 128), jnp.float32)
    if cols_n % 128:
        lane = lax.broadcasted_iota(jnp.int32, (tok, 128), 1)
        logits[:, (nt - 1) * 128:] = jnp.where(lane < cols_n % 128, 0.0, -1e30)
    for j in range(1, ndp):
        tp_copy(j, lax.rem(d + ndp - j, ndp)).wait_recv()

    offset = (me * cols_n).astype(jnp.float32)
    na = sp.shape[0] // tok
    iota_a = lax.broadcasted_iota(jnp.int32, (na, 128), 0)
    iota_b = lax.broadcasted_iota(jnp.int32, (128, 128), 0)
    lane8 = lax.broadcasted_iota(jnp.int32, (8, 128), 1)

    def build(step, _):
        t0 = pl.multiple_of(step * 8, 8)
        both = tp_all[pl.ds(t0, 8), :]
        turned = pltpu.roll(both, top_n, 1)
        ids = jnp.where(lane8 < top_n, both, turned)
        probs = jnp.where(lane8 < top_n, turned, both)
        high = probs.astype(jnp.bfloat16).astype(jnp.float32)
        parts = jnp.where(lane8 < top_n, high, probs - high)
        local = (ids - offset).astype(jnp.int32)
        inside = (local >= 0) & (local < cols_n)
        tile = jnp.where(inside, local >> 7, -1)
        low = local & 127
        for r in range(8):
            left = jnp.where(iota_a == tile[r:r + 1, :], parts[r:r + 1, :], 0.0)
            right = jnp.where(iota_b == low[r:r + 1, :], 1.0, 0.0)
            sp[pl.ds(t0 + r, na, stride=tok), :] = lax.dot_general(
                left.astype(jnp.bfloat16), right.astype(jnp.bfloat16), NT,
                preferred_element_type=jnp.float32)
        return 0

    lax.fori_loop(0, tok // 8, build, 0)

    def forward_in(c):
        for j in range(1, nx):
            hx_in(j, c).wait_recv()
            hc_copy(j, c).start()

    l_copy().wait()
    forward_in(0)
    wide = 512

    def first(c, _):
        @pl.when(c + 1 < nk)
        def _():
            forward_in(c + 1)

        for j in range(nx):
            hc_in(j, c).wait_recv()
        w_copy(c).wait()
        hc = h_all[:, kpart(c)]
        for n0 in range(0, cols_n, wide):
            n1 = min(n0 + wide, cols_n)
            logits[:, n0:n1] += lax.dot_general(
                hc, wv[n0:n1, kpart(c)], NT, preferred_element_type=jnp.float32)
        return 0

    lax.fori_loop(0, nk, first, 0)

    deep = 32
    lane_deep = lax.broadcasted_iota(jnp.int32, (deep, 128), 1)

    def peak(step, _):
        t0 = pl.multiple_of(step * deep, deep)
        ts = pl.ds(t0, deep)
        top = logits[ts, 0:128]
        for a in range(1, nt):
            top = jnp.maximum(top, logits[ts, a * 128:(a + 1) * 128])
        m = jnp.max(top, axis=1, keepdims=True)
        total = jnp.zeros((deep, 128), jnp.float32)
        picked = jnp.zeros((deep, 128), jnp.float32)
        for a in range(nt):
            value = logits[ts, a * 128:(a + 1) * 128]
            picked += value * sp[pl.ds(a * tok + t0, deep), :]
            e = jnp.exp(value - m)
            logits[ts, a * 128:(a + 1) * 128] = e
            total += e
        s = jnp.sum(total, axis=1, keepdims=True)
        q = jnp.sum(picked, axis=1, keepdims=True)
        cols[ts, :] = jnp.where(lane_deep == 0, m, jnp.where(lane_deep == 1, s, q))
        return 0

    lax.fori_loop(0, tok // deep, peak, 0)

    turned_stats = cols[...].T
    for j in range(tok // 128):
        stats[me, 3 * j:3 * j + 3, :] = turned_stats[0:3, j * 128:(j + 1) * 128]
    for j in range(1, nd):
        st_copy(j, me).start()
    back[...] = jnp.zeros_like(back)
    for j in range(1, nd):
        st_copy(j, lax.rem(me + nd - j, nd)).wait_recv()
    for j in range(tok // 128):
        part = slice(j * 128, (j + 1) * 128)
        ms = stats[:, 3 * j, :]
        big = jnp.max(ms, axis=0, keepdims=True)
        z = jnp.sum(stats[:, 3 * j + 1, :] * jnp.exp(ms - big), axis=0, keepdims=True)
        back[0:1, part] = big + jnp.log(z)
        back[1:2, part] = jnp.sum(stats[:, 3 * j + 2, :], axis=0, keepdims=True)
    cols2[...] = back[...].T

    lane16 = lax.broadcasted_iota(jnp.int32, (16, 128), 1)

    def grad(step, _):
        t0 = pl.multiple_of(step * 16, 16)
        ts = pl.ds(t0, 16)
        mass = jnp.sum(jnp.where(lane16 >= top_n, tp_all[ts, :], 0.0), axis=1, keepdims=True)
        scale = mass * jnp.exp(cols[ts, 0:1] - cols2[ts, 0:1])
        for a in range(nt):
            n1 = min(128, cols_n - a * 128)
            value = logits[ts, a * 128:(a + 1) * 128] * scale - sp[pl.ds(a * tok + t0, 16), :]
            lg[ts, a * 128:a * 128 + n1] = value[:, :n1].astype(jnp.bfloat16)
        return 0

    lax.fori_loop(0, tok // 16, grad, 0, unroll=2)

    def pair_sum(i, jx):
        g1_copy(i, jx).wait_recv()
        return g[i, block(2 * lax.rem(x + jx, nx) + core), :] + r1[i, jx]

    def to_x(i):
        for jx in range(1, nx):
            sx[i, jx - 1] = pair_sum(i, jx).astype(jnp.bfloat16)
            gx_copy(i, jx).start()

    def to_vocab(i, last):
        both = pair_sum(i, 0)
        for jx in range(1, nx):
            gx_copy(i, jx).wait_recv()
            both += rx[i, jx - 1].astype(jnp.float32)
        for m in range(q):
            def send_block():
                s2[i, m] = both[:, starts[m]:starts[m] + ww].astype(jnp.bfloat16)
                g2_copy(i, m).start()

            if last:
                @pl.when(m == mm)
                def _():
                    own[...] = both[:, starts[m]:starts[m] + ww]

                pl.when(m != mm)(send_block)
            else:
                send_block()

    def second(i, _):
        part = pl.ds(pl.multiple_of(lax.rem(mg + 1 + i, ng) * group, group), group)
        g[i] = jnp.dot(lg[...], wv[:, part], preferred_element_type=jnp.float32)
        for jx in range(nx):
            g1_copy(i, jx).start()

        @pl.when(i > 0)
        def _():
            to_x(i - 1)

        @pl.when(i > 1)
        def _():
            to_vocab(i - 2, False)

        return 0

    lax.fori_loop(0, ng, second, 0)
    to_x(ng - 1)
    if ng > 1:
        to_vocab(ng - 2, False)
    to_vocab(ng - 1, True)

    def not_own(i, m):
        return (m != mm) if i == ng - 1 else (mm >= 0)

    mine = block(d)
    lane = lax.broadcasted_iota(jnp.int32, (rows, 128), 1)
    probs = jnp.where(lane >= top_n, tp_all[mine, :], 1.0)
    entropy = jnp.sum(probs * jnp.log(probs), axis=1, keepdims=True)
    mass = jnp.sum(jnp.where(lane >= top_n, probs, 0.0), axis=1, keepdims=True)
    diagonal = lax.broadcasted_iota(jnp.int32, (rows, rows), 0) == (
        lax.broadcasted_iota(jnp.int32, (rows, rows), 1))
    column = entropy - cols2[mine, 1:2] + mass * cols2[mine, 0:1]
    div_out[...] = jnp.sum(jnp.where(diagonal, column, 0.0), axis=0, keepdims=True)
    weight = jnp.sum(jnp.where(diagonal, tw[...], 0.0), axis=1, keepdims=True)

    for i in range(ng):
        for m in range(q):
            @pl.when(not_own(i, m))
            def _():
                g2_in(i, m).wait_recv()
                own[...] += r2[i, m].astype(jnp.float32)
    for m in range(q):
        @pl.when(m == mm)
        def _():
            lo = m * feat - starts[m]
            grad_out[...] = own[:, lo:lo + feat] * weight

    for c in range(nk):
        for j in range(1, nx):
            hx_copy(j, c).wait_send()
        for j in range(nx):
            hc_copy(j, c).wait_send()
    for j in range(1, ndp):
        tp_copy(j, d).wait_send()
    for j in range(1, nd):
        st_copy(j, me).wait_send()
    for i in range(ng):
        for jx in range(nx):
            g1_copy(i, jx).wait_send()
        for jx in range(1, nx):
            gx_copy(i, jx).wait_send()
        for m in range(q):
            @pl.when(not_own(i, m))
            def _():
                g2_copy(i, m).wait_send()


def body(ndp, nv, hidden, head_weight, teacher_ids, teacher_probs, token_weight):
    rows, depth = hidden.shape
    cols_n = head_weight.shape[1]
    tok, nx, nd, feat = rows * ndp, ndp // 2, ndp * nv, depth // nv
    q, ww, _ = windows(feat)
    ng, group = nv // q, q * feat
    kc = next(k for k in (512, 256, 128) if depth % k == 0)
    nk = depth // kc
    nt = (cols_n + 127) // 128
    na = (nt + 7) // 8 * 8
    srows = (3 * (tok // 128) + 7) // 8 * 8
    f32, bf16, dma = jnp.float32, jnp.bfloat16, pltpu.SemaphoreType.DMA
    anyspace = pl.BlockSpec(memory_space=pl.ANY)
    vmem = pl.BlockSpec(memory_space=pltpu.VMEM)
    div, out = pl.pallas_call(
        functools.partial(kernel, ndp, nv, kc),
        out_shape=(
            jax.ShapeDtypeStruct((1, rows), f32), jax.ShapeDtypeStruct((rows, feat), f32)),
        in_specs=[anyspace, anyspace, vmem, vmem, vmem],
        out_specs=(vmem, vmem),
        scratch_shapes=[
            pltpu.VMEM((cols_n, depth), bf16), pltpu.VMEM((tok, depth), bf16),
            pltpu.VMEM((tok, 128), f32), pltpu.VMEM((na * tok, 128), f32),
            pltpu.VMEM((tok, nt * 128), f32), pltpu.VMEM((tok, cols_n), bf16),
            pltpu.VMEM((ng, tok, group), f32), pltpu.VMEM((ng, nx, rows, group), f32),
            pltpu.VMEM((ng, nx - 1, rows, group), bf16),
            pltpu.VMEM((ng, nx - 1, rows, group), bf16),
            pltpu.VMEM((ng, q, rows, ww), bf16), pltpu.VMEM((ng, q, rows, ww), bf16),
            pltpu.VMEM((nd, srows, 128), f32), pltpu.VMEM((tok, 128), f32),
            pltpu.VMEM((tok, 128), f32), pltpu.VMEM((128, tok), f32),
            pltpu.VMEM((rows, ww), f32),
            dma((nk,)), dma((1,)), dma((nx - 1, nk)), dma((nx - 1, nk)),
            dma((nx, nk)), dma((nx, nk)), dma((ndp - 1,)), dma((ndp - 1,)),
            dma((nd - 1,)), dma((nd - 1,)), dma((ng, nx)), dma((ng, nx)),
            dma((ng, nx - 1)), dma((ng, nx - 1)), dma((ng, q)), dma((ng, q)),
        ],
        compiler_params=pltpu.CompilerParams(
            collective_id=0, has_side_effects=True, vmem_limit_bytes=67043328),
    )(hidden, head_weight.T, teacher_ids, teacher_probs, token_weight[None, :])
    return div[0], out


def solution(mesh):
    in_specs = (P("dp", None), P(None, ("dp", "vocab")), P("dp", None), P("dp", None), P("dp"))
    out_specs = (P("dp"), P("dp", "vocab"))
    return jax.shard_map(
        functools.partial(body, mesh.shape["dp"], mesh.shape["vocab"]),
        mesh=mesh, in_specs=in_specs, out_specs=out_specs, check_vma=False)
```

profile of v0, /device:TPU:0, one launch (start us, length us, event | category | flops | bytes accessed | tf_op | source)
XLA Modules:
  0.0 73.2 jit_solution(17403787428273358504)
XLA Ops:
  0.6 69.8 %shard_map.68 = (f32[1,64]{1,0:T(1,128)}, f32[64,448]{1,0:T(8,128)}) custom-call(bf16[64,3584]{1,0:T(8,128)(2,1)} %hid.1, bf16[4752,3584]{1,0:T(8,128)(2,1)} %bitcast.3, s32[64,64]{1,0:T(8,128)} %ids_in.1, f32[64,64]{1,0:T(8,128)} %probs_in.1, f32[1,64]{1,0:T(1,128)} %bitcast.4), custom_call_target="tpu_custom_call" | custom-call | tf_op jit(solution)/shard_map/pallas_call | solution.py:378
  70.4 1.2 %copy.9 = f32[64]{0:T(128)} copy(f32[64]{0:T(128)} %bitcast.5) | data formatting | bytes 512
  71.6 1.6 %copy.10 = f32[64,448]{1,0:T(8,128)} copy(f32[64,448]{1,0:T(8,128)} %get-tuple-element.9) | data formatting | bytes 229376
where the time goes:
time: 73.4 us; the launch traced here: 73.2 us
  Pallas kernels  69.8 us (95%)
  local copies, waits for them, and re-layouts  2.74 us (4%)
    pallas_call x1, Pallas kernels, body(): pl.pallas_call(functools.partial(kernel, ndp, nv, kc), out_shape=(jax.Sha...  69.8 us
    unnamed x2, local copies, waits for them, and re-layouts  2.74 us

commit v1 on v0

v1 whole, which is shorter than its diff:
```python
import functools

import jax
import jax.numpy as jnp
from jax import lax
from jax.experimental import pallas as pl
from jax.experimental.pallas import tpu as pltpu
from jax.sharding import PartitionSpec as P

MESH = pl.DeviceIdType.MESH
NT = (((1,), (1,)), ((), ()))


def windows(feat):
    q = next(k for k in (1, 2, 4, 8, 16, 32, 64, 128) if k * feat % 128 == 0)
    first = [m * feat // 128 * 128 for m in range(q)]
    ww = max((m + 1) * feat - first[m] + 127 for m in range(q)) // 128 * 128
    return q, ww, [min(f, q * feat - ww) for f in first]


def spans(depth):
    wide = next(k for k in (512, 256, 128) if depth % k == 0)
    return [(first, wide) for first in range(0, depth, wide)]


def runs_of(depth, feat):
    q, ww, starts = windows(feat)
    out = []
    for b in range(depth // (q * feat)):
        for m in range(q):
            a = b * q * feat + starts[m]
            for i, (first, width) in enumerate(spans(depth)):
                lo, hi = max(a, first), min(a + ww, first + width)
                if lo < hi:
                    out.append((i, b, m, lo - first, lo - a, hi - lo))
    return out


def kernel(
    ndp, nv, hid, w, ids_in, probs_in, tw, div_out, grad_out,
    wv, h_all, ids_v, probs_v, tw_v, tp_all, sp, lt, logits, lg, g, r1, sx, rx, s2, r2, sb, rb, rz,
    stats, picks, cols, cols2, back, own,
    w_sem, l_sem, i_sem, pk_s, pk_r, hx_s, hx_r, hc_s, hc_r, tp_s, tp_r, st_s, st_r,
    g1_s, g1_r, gx_s, gx_r, g2_s, g2_r, gb_s, gb_r, rz_s, rz_r,
):
    d, mv = lax.axis_index("dp"), lax.axis_index("vocab")
    x, core = d // 2, d % 2
    nx, nd = ndp // 2, ndp * nv
    me = d * nv + mv
    rows, depth = hid.shape
    cols_n = w.shape[0]
    tok = rows * ndp
    parts = spans(depth)
    nk = ng = len(parts)
    nt = (cols_n + 127) // 128
    nb = tok // 128
    feat = depth // nv
    q, ww, starts = windows(feat)
    nblk, group = nv // q, q * feat
    runs = runs_of(depth, feat)
    direct = [i >= ng - 4 for i in range(ng)]
    shift = sorted(range(nblk), key=lambda o: (-min(o, nblk - o), o))
    passed = nblk == 4 and parts[ng - 4][0] <= 2 * group
    early = [run for run in runs if not direct[run[0]] and not (passed and run[1] == 0)]
    late = [run for run in runs if direct[run[0]]]
    mg, mm = mv // q, lax.rem(mv, q)
    other = (2 * x + 1 - core, mv)

    def block(dp_index):
        return pl.ds(pl.multiple_of(dp_index * rows, rows), rows)

    def drain(ref, sem):
        pltpu.make_async_copy(ref, ref, sem).wait()

    def strip(width):
        units = rows * width // (8 * 128)
        tall = next(k for k in range(1, cols_n // 8 + 1)
                    if units % k == 0 and units // k <= depth // 128)
        return wv.at[0:tall * 8, 0:units // tall * 128]

    cuts = sorted({first for first, _ in parts} | set(range(0, depth, group)) | {depth})
    pieces = list(zip(cuts[:-1], cuts[1:]))

    def pair_of(b):
        return lax.rem(mg + shift[b], nblk)

    def source(lo, hi):
        begin = pair_of(lo // group) * group + lo % group
        return pl.ds(pl.multiple_of(begin, 128), hi - lo)

    def kpart(c):
        return pl.ds(*parts[c])

    def w_piece(lo, hi):
        c = max(c for c in range(nk) if parts[c][0] <= lo)
        return pltpu.make_async_copy(
            w.at[:, source(lo, hi)], wv.at[:, lo:hi], w_sem.at[c])

    def l_piece(b):
        lo, hi = b * group, (b + 1) * group
        return pltpu.make_async_copy(
            hid.at[:, source(lo, hi)], h_all.at[block(d), lo:hi], l_sem.at[0])

    def hx_copy(j, c):
        return pltpu.make_async_remote_copy(
            src_ref=h_all.at[block(d), kpart(c)], dst_ref=h_all.at[block(d), kpart(c)],
            send_sem=hx_s.at[0], recv_sem=hx_r.at[c],
            device_id=(2 * lax.rem(x + j, nx) + core, mv), device_id_type=MESH)

    def hc_copy(j, c):
        src = h_all.at[block(2 * lax.rem(x + nx - j, nx) + core), kpart(c)]
        return pltpu.make_async_remote_copy(
            src_ref=src, dst_ref=src,
            send_sem=hc_s.at[0], recv_sem=hc_r.at[c],
            device_id=other, device_id_type=MESH)

    def tp_copy(to, near):
        return pltpu.make_async_remote_copy(
            src_ref=tp_all.at[block(d), :], dst_ref=tp_all.at[block(d), :],
            send_sem=tp_s.at[0], recv_sem=tp_r.at[0 if near else 1],
            device_id=(to, mv), device_id_type=MESH)

    def st_copy(j, sender):
        to = lax.rem(me + j, nd)
        return pltpu.make_async_remote_copy(
            src_ref=stats.at[sender, 0:2 * nb], dst_ref=stats.at[sender, 0:2 * nb],
            send_sem=st_s.at[0], recv_sem=st_r.at[0],
            device_id=(to // nv, lax.rem(to, nv)), device_id_type=MESH)

    def pk_copy(j, sender):
        to = lax.rem(me + j, nd)
        return pltpu.make_async_remote_copy(
            src_ref=picks.at[sender, 0:nb], dst_ref=picks.at[sender, 0:nb],
            send_sem=pk_s.at[0], recv_sem=pk_r.at[0],
            device_id=(to // nv, lax.rem(to, nv)), device_id_type=MESH)

    def small_in(i):
        src, dst = ((ids_in, ids_v), (probs_in, probs_v), (tw, tw_v))[i]
        return pltpu.make_async_copy(src, dst, i_sem.at[i])

    def g1_copy(i, jx):
        theirs = block(2 * lax.rem(x + jx, nx) + 1 - core)
        width = parts[i][1]
        return pltpu.make_async_remote_copy(
            src_ref=g.at[i, theirs, 0:width], dst_ref=r1.at[i, jx, :, 0:width],
            send_sem=g1_s.at[0], recv_sem=g1_r.at[i],
            device_id=other, device_id_type=MESH)

    def gx_copy(i, jx):
        width = parts[i][1]
        return pltpu.make_async_remote_copy(
            src_ref=sx.at[i, jx - 1, :, 0:width], dst_ref=rx.at[i, jx - 1, :, 0:width],
            send_sem=gx_s.at[0], recv_sem=gx_r.at[i],
            device_id=(2 * lax.rem(x + jx, nx) + core, mv), device_id_type=MESH)

    def g2_copy(run):
        i, b, m, at, to, width = run
        return pltpu.make_async_remote_copy(
            src_ref=s2.at[i, :, at:at + width], dst_ref=r2.at[b * q + mm, :, to:to + width],
            send_sem=g2_s.at[0], recv_sem=g2_r.at[0],
            device_id=(d, pair_of(b) * q + m), device_id_type=MESH)

    def rz_copy(i):
        first, width = parts[i]
        width = min(width, group - first)
        return pltpu.make_async_remote_copy(
            src_ref=s2.at[i, :, 0:width], dst_ref=rz.at[:, first:first + width],
            send_sem=rz_s.at[0], recv_sem=rz_r.at[0],
            device_id=(d, lax.rem(mg + nblk - 1, nblk) * q + mm), device_id_type=MESH)

    def gb_copy(run, jx):
        i, b, m, at, to, width = run
        return pltpu.make_async_remote_copy(
            src_ref=sb.at[i, jx, :, at:at + width], dst_ref=rb.at[(jx * nblk + b) * q + mm, :, to:to + width],
            send_sem=gb_s.at[0], recv_sem=gb_r.at[0],
            device_id=(2 * lax.rem(x + jx, nx) + core, pair_of(b) * q + m), device_id_type=MESH)

    for b in range(nblk):
        l_piece(b).start()
    for i in range(3):
        small_in(i).start()

    barrier = pltpu.get_barrier_semaphore()

    def greet(j, _):
        to = lax.rem(me + j, nd)
        pl.semaphore_signal(
            barrier, inc=1, device_id=(to // nv, lax.rem(to, nv)), device_id_type=MESH)
        return 0

    lax.fori_loop(1, nd, greet, 0)
    for lo, hi in pieces:
        w_piece(lo, hi).start()

    top_n = ids_in.shape[1]
    for i in range(3):
        small_in(i).wait()
    tp_all[block(d), 0:top_n] = ids_v[...].astype(jnp.float32)
    tp_all[block(d), top_n:2 * top_n] = probs_v[...]
    drain(h_all.at[block(d), :], l_sem.at[0])
    pl.semaphore_wait(barrier, nd - 1)

    for j in range(1, nx):
        hx_copy(j, 0).start()
    tp_copy(other[0], True).start()
    for c in range(nk):
        hc_copy(0, c).start()
        if c > 0:
            for j in range(1, nx):
                hx_copy(j, c).start()
    for j in range(1, nx):
        for side in range(2):
            tp_copy(2 * lax.rem(x + j, nx) + side, False).start()

    offset = (me * cols_n).astype(jnp.float32)
    nh = (cols_n + 255) // 256
    lane8 = lax.broadcasted_iota(jnp.int32, (8, 128), 1)
    sub8 = lax.broadcasted_iota(jnp.int32, (8, 128), 0)
    first8 = lane8 < top_n
    lo_iota = lax.broadcasted_iota(jnp.int32, (256, 128), 0)

    def build_group(t0):
        both = tp_all[pl.ds(t0, 8), :]
        turned = pltpu.roll(both, top_n, 1)
        ids = jnp.where(first8, both, turned)
        probs = jnp.where(first8, turned, both)
        high = probs.astype(jnp.bfloat16).astype(jnp.float32)
        rest = probs - high
        local = (ids - offset).astype(jnp.int32)
        inside = (local >= 0) & (local < cols_n)
        tile = jnp.where(inside, local >> 8, -1)
        low = local & 255
        left, right = [], []
        for u in range(4):
            tile_u = jnp.where(sub8 == jnp.where(first8, 2 * u, 2 * u + 1), tile, -1)
            left.append(jnp.concatenate(
                [jnp.where(tile_u == h, part, 0.0) for part in (high, rest) for h in range(nh)],
                axis=0).astype(jnp.bfloat16))
            low_u = jnp.where(first8[0:1], low[2 * u:2 * u + 1, :], low[2 * u + 1:2 * u + 2, :])
            right.append(jnp.where(lo_iota == low_u, 1.0, 0.0).astype(jnp.bfloat16))
        out = lax.dot_general(
            jnp.concatenate(left, axis=1), jnp.concatenate(right, axis=1), NT,
            preferred_element_type=jnp.float32)
        for h in range(nh):
            sp[pl.ds(t0, 8), h * 256:(h + 1) * 256] = (
                out[h * 8:(h + 1) * 8, :] + out[(nh + h) * 8:(nh + h + 1) * 8, :])
        mass = jnp.sum(jnp.where(first8, 0.0, both), axis=1, keepdims=True)
        cols[pl.ds(t0, 8), :] = jnp.broadcast_to(jnp.log(mass), (8, 128))

    deal = 4

    def build_block(dp_index):
        def build(step, _):
            for r in range(deal):
                build_group(pl.multiple_of(dp_index * rows + step * 8 * deal + 8 * r, 8))
            return 0

        lax.fori_loop(0, rows // (8 * deal), build, 0)

    build_block(d)
    drain(tp_all.at[block(d), :], tp_r.at[0])
    build_block(other[0])
    lt[(nt - 1) * 128:, :] = jnp.full((128, tok), -1e30, jnp.float32)

    def forward_in(c):
        first, width = parts[c]
        drain(h_all.at[0:(nx - 1) * rows, kpart(c)], hx_r.at[c])
        for j in range(1, nx):
            hc_copy(j, c).start()

    forward_in(0)
    halves = 2 * ((cols_n + 1023) // 1024)
    wide = ((cols_n + halves - 1) // halves + 15) // 16 * 16
    top = jnp.full((8, tok), -3e38, jnp.float32)
    turned_tiles = 0
    for c in range(nk):
        if c + 1 < nk:
            forward_in(c + 1)
        drain(h_all.at[0:nx * rows, kpart(c)], hc_r.at[c])
        drain(wv.at[:, kpart(c)], w_sem.at[c])
        hc = h_all[:, kpart(c)]
        for n0 in range(0, cols_n, wide):
            n1 = min(n0 + wide, cols_n)
            new = lax.dot_general(
                wv[n0:n1, kpart(c)], hc, NT, preferred_element_type=jnp.float32)
            if c == 0:
                lt[n0:n1, :] = new
            else:
                lt[n0:n1, :] += new
            if c == nk - 1:
                ready = nt if n1 == cols_n else n0 // 128
                for a in range(turned_tiles, ready):
                    value = lt[a * 128:(a + 1) * 128, :]
                    logits[:, a * 128:(a + 1) * 128] = value.T
                    for r in range(16):
                        top = jnp.maximum(top, value[8 * r:8 * r + 8, :])
                turned_tiles = max(turned_tiles, ready)

    m = jnp.max(top, axis=0, keepdims=True)
    deep = next(k for k in (304, 160, 152, 80, 64, 32, 16, 8) if nt * 128 % k == 0)

    def expsum(step, total):
        n0 = pl.multiple_of(step * deep, 8)
        for r in range(deep // 8):
            total += jnp.exp(lt[pl.ds(n0 + 8 * r, 8), :] - m)
        return total

    total = lax.fori_loop(0, nt * 128 // deep, expsum, jnp.zeros((8, tok), jnp.float32))
    s = jnp.sum(total, axis=0, keepdims=True)

    for j in range(nb):
        stats[me, j:j + 1, :] = m[:, j * 128:(j + 1) * 128]
        stats[me, nb + j:nb + j + 1, :] = s[:, j * 128:(j + 1) * 128]
    for j in range(1, nd):
        st_copy(j, me).start()
    drain(tp_all.at[0:(ndp - 2) * rows, :], tp_r.at[1])
    for j in range(1, nx):
        for side in range(2):
            build_block(2 * lax.rem(x + j, nx) + side)
    back[...] = jnp.zeros_like(back)

    drain(stats.at[0:nd - 1, 0:2 * nb], st_r.at[0])
    for j in range(nb):
        part = slice(j * 128, (j + 1) * 128)
        ms = stats[:, j, :]
        big = jnp.max(ms, axis=0, keepdims=True)
        z = jnp.sum(stats[:, nb + j, :] * jnp.exp(ms - big), axis=0, keepdims=True)
        back[0:1, part] = big + jnp.log(z)
    cols2[...] = back[...].T


    def grad(step, _):
        t0 = pl.multiple_of(step * 16, 16)
        ts = pl.ds(t0, 16)
        shift = cols2[ts, 0:1] - cols[ts, 0:1]
        picked = jnp.zeros((16, 128), jnp.float32)
        for a in range(nt):
            n1 = min(128, cols_n - a * 128)
            value = logits[ts, a * 128:(a + 1) * 128]
            sparse = sp[ts, a * 128:(a + 1) * 128]
            picked += value * sparse
            lg[ts, a * 128:a * 128 + n1] = (
                jnp.exp(value - shift) - sparse)[:, :n1].astype(jnp.bfloat16)
        cols[ts, :] = picked
        return 0

    lax.fori_loop(0, tok // 16, grad, 0, unroll=2)

    def pair_sum(i, jx):
        mine_rows, width = block(2 * lax.rem(x + jx, nx) + core), parts[i][1]
        return g[i, mine_rows, 0:width] + r1[i, jx, :, 0:width]

    def to_x(i):
        width = parts[i][1]
        drain(r1.at[i, :, :, 0:width], g1_r.at[i])
        if direct[i]:
            for jx in list(range(1, nx)) + [0]:
                both = pair_sum(i, jx)
                sb[i, jx, :, 0:width] = both.astype(jnp.bfloat16)
                for run in late:
                    _, b, m, at, to, wide = run
                    if run[0] != i or (jx == 0 and passed and b == 2):
                        continue
                    if jx == 0 and b == nblk - 1:
                        @pl.when(m == mm)
                        def _():
                            own[:, to:to + wide] = both[:, at:at + wide]

                        pl.when(m != mm)(gb_copy(run, jx).start)
                    else:
                        gb_copy(run, jx).start()
            return
        for jx in range(1, nx):
            sx[i, jx - 1, :, 0:width] = pair_sum(i, jx).astype(jnp.bfloat16)
            gx_copy(i, jx).start()

    def to_vocab(i):
        if direct[i]:
            return
        width = parts[i][1]
        both = pair_sum(i, 0)
        drain(rx.at[i, :, :, 0:width], gx_r.at[i])
        for jx in range(1, nx):
            both += rx[i, jx - 1, :, 0:width].astype(jnp.float32)
        s2[i, :, 0:width] = both.astype(jnp.bfloat16)
        if passed and parts[i][0] < group:
            rz_copy(i).start()
        for run in early:
            _, b, m, at, to, wide = run
            if run[0] != i:
                continue
            if b == nblk - 1:
                @pl.when(m == mm)
                def _():
                    own[:, to:to + wide] = both[:, at:at + wide]

                pl.when(m != mm)(g2_copy(run).start)
            else:
                g2_copy(run).start()

    lag = 3
    for i in range(ng):
        first, width = parts[i]
        g[i, :, 0:width] = jnp.dot(
            lg[...], wv[:, first:first + width], preferred_element_type=jnp.float32)
        for jx in range(nx):
            g1_copy(i, jx).start()
        if i >= 1:
            to_x(i - 1)
        if i >= lag:
            to_vocab(i - lag)
        if i == 2 or (ng < 3 and i == ng - 1):
            turned = jnp.sum(cols[...].T, axis=0, keepdims=True)
            for j in range(nb):
                picks[me, j:j + 1, :] = turned[:, j * 128:(j + 1) * 128]
            for j in range(1, nd):
                pk_copy(j, me).start()

    to_x(ng - 1)
    for i in range(max(ng - lag, 0), ng):
        to_vocab(i)

    if passed:
        drain(rz, rz_r.at[0])
        for i in range(ng):
            first, width = parts[i]
            lo, hi = max(first, 2 * group) - first, min(first + width, 3 * group) - first
            if lo >= hi:
                continue
            mine_rows, at = block(2 * x + core), first + lo - 2 * group
            sb[i, 0, :, lo:hi] = (
                g[i, mine_rows, lo:hi] + r1[i, 0, :, lo:hi]
                + rz[:, at:at + hi - lo].astype(jnp.float32)).astype(jnp.bfloat16)
            for run in late:
                if run[0] == i and run[1] == 2:
                    gb_copy(run, 0).start()

    drain(picks.at[0:nd - 1, 0:nb], pk_r.at[0])
    for j in range(nb):
        back[1:2, j * 128:(j + 1) * 128] = jnp.sum(picks[:, j, :], axis=0, keepdims=True)
    cols2[...] = back[...].T
    mine = block(d)
    lane = lax.broadcasted_iota(jnp.int32, (rows, 128), 1)
    probs = jnp.where(lane >= top_n, tp_all[mine, :], 1.0)
    entropy = jnp.sum(probs * jnp.log(probs), axis=1, keepdims=True)
    mass = jnp.sum(jnp.where(lane >= top_n, probs, 0.0), axis=1, keepdims=True)
    diagonal = lax.broadcasted_iota(jnp.int32, (rows, rows), 0) == (
        lax.broadcasted_iota(jnp.int32, (rows, rows), 1))
    column = entropy - cols2[mine, 1:2] + mass * cols2[mine, 0:1]
    div_out[...] = jnp.sum(jnp.where(diagonal, column, 0.0), axis=0, keepdims=True)
    weight = jnp.sum(jnp.where(diagonal, tw_v[...], 0.0), axis=1, keepdims=True)

    for m in range(q):
        @pl.when(m == mm)
        def _():
            def arrivals(some, senders):
                return [(run, s) for run in some if run[2] == m for s in senders
                        if run[1] < nblk - 1 or s != m]

            def width_of(some):
                return sum(run[5] for run, _ in some)

            near = arrivals(early, range(q))
            if near:
                drain(strip(width_of(near)), g2_r.at[0])
            for (_, b, _, _, to, width), s in near:
                own[:, to:to + width] += r2[b * q + s, :, to:to + width].astype(jnp.float32)
            far = [(run, (jx * nblk + run[1]) * q + s)
                   for run in late if run[2] == m for jx in range(nx) for s in range(q)
                   if jx > 0 or run[1] < nblk - 1 or s != m]
            if far:
                drain(strip(width_of(far)), gb_r.at[0])
            for (_, b, _, _, to, width), s in far:
                own[:, to:to + width] += rb[s, :, to:to + width].astype(jnp.float32)
            lo = m * feat - starts[m]
            grad_out[...] = own[:, lo:lo + feat] * weight
            sent = sum(run[5] for run in early if run[1] < nblk - 1 or run[2] != m)
            if sent:
                drain(strip(sent), g2_s.at[0])
            sent = sum(run[5] for run in late for jx in range(nx)
                       if jx > 0 or run[1] < nblk - 1 or run[2] != m)
            if late:
                drain(strip(sent), gb_s.at[0])

    drain(h_all.at[0:(nx - 1) * rows, :], hx_s.at[0])
    drain(h_all.at[0:nx * rows, :], hc_s.at[0])
    drain(tp_all.at[0:(ndp - 1) * rows, :], tp_s.at[0])
    drain(stats.at[0:nd - 1, 0:2 * nb], st_s.at[0])
    if passed:
        drain(rz, rz_s.at[0])
    drain(picks.at[0:nd - 1, 0:nb], pk_s.at[0])
    drain(g.at[0:depth // g.shape[2], 0:nx * rows, :], g1_s.at[0])
    drain(strip((nx - 1) * sum(p[1] for p, far in zip(parts, direct) if not far)), gx_s.at[0])


def body(ndp, nv, hidden, head_weight, teacher_ids, teacher_probs, token_weight):
    rows, depth = hidden.shape
    cols_n = head_weight.shape[1]
    tok, nx, nd, feat = rows * ndp, ndp // 2, ndp * nv, depth // nv
    q, ww, _ = windows(feat)
    gw = max(width for _, width in spans(depth))
    nk = ng = len(spans(depth))
    nt = (cols_n + 127) // 128
    nh = (cols_n + 255) // 256
    srows = (2 * (tok // 128) + 7) // 8 * 8
    prows = (tok // 128 + 7) // 8 * 8
    f32, bf16, dma = jnp.float32, jnp.bfloat16, pltpu.SemaphoreType.DMA
    anyspace = pl.BlockSpec(memory_space=pl.ANY)
    vmem = pl.BlockSpec(memory_space=pltpu.VMEM)
    div, out = pl.pallas_call(
        functools.partial(kernel, ndp, nv),
        out_shape=(
            jax.ShapeDtypeStruct((1, rows), f32), jax.ShapeDtypeStruct((rows, feat), f32)),
        in_specs=[anyspace] * 5,
        out_specs=(vmem, vmem),
        scratch_shapes=[
            pltpu.VMEM((cols_n, depth), bf16), pltpu.VMEM((tok, depth), bf16),
            pltpu.VMEM(teacher_ids.shape, jnp.int32), pltpu.VMEM(teacher_probs.shape, f32),
            pltpu.VMEM((1, rows), f32),
            pltpu.VMEM((tok, 128), f32), pltpu.VMEM((tok, nh * 256), f32),
            pltpu.VMEM((nt * 128, tok), f32),
            pltpu.VMEM((tok, nt * 128), f32), pltpu.VMEM((tok, cols_n), bf16),
            pltpu.VMEM((ng, tok, gw), f32), pltpu.VMEM((ng, nx, rows, gw), f32),
            pltpu.VMEM((ng, nx - 1, rows, gw), bf16),
            pltpu.VMEM((ng, nx - 1, rows, gw), bf16),
            pltpu.VMEM((ng, rows, gw), bf16), pltpu.VMEM((nv, rows, ww), bf16),
            pltpu.VMEM((ng, nx, rows, gw), bf16), pltpu.VMEM((nx * nv, rows, ww), bf16), pltpu.VMEM((rows, q * feat), bf16),
            pltpu.VMEM((nd, srows, 128), f32), pltpu.VMEM((nd, prows, 128), f32),
            pltpu.VMEM((tok, 128), f32), pltpu.VMEM((tok, 128), f32),
            pltpu.VMEM((128, tok), f32), pltpu.VMEM((rows, ww), f32),
            dma((nk,)), dma((1,)), dma((3,)), dma((1,)), dma((1,)),
            dma((1,)), dma((nk,)), dma((1,)), dma((nk,)), dma((1,)), dma((2,)),
            dma((1,)), dma((1,)), dma((1,)), dma((ng,)), dma((1,)), dma((ng,)),
            dma((1,)), dma((1,)), dma((1,)), dma((1,)), dma((1,)), dma((1,)),
        ],
        compiler_params=pltpu.CompilerParams(
            collective_id=0, has_side_effects=True, vmem_limit_bytes=67043328),
    )(hidden, head_weight.T, teacher_ids, teacher_probs, token_weight[None, :])
    return div[0], out


def solution(mesh):
    in_specs = (P("dp", None), P(None, ("dp", "vocab")), P("dp", None), P("dp", None), P("dp"))
    out_specs = (P("dp"), P("dp", "vocab"))
    return jax.shard_map(
        functools.partial(body, mesh.shape["dp"], mesh.shape["vocab"]),
        mesh=mesh, in_specs=in_specs, out_specs=out_specs, check_vma=False)
```

time: 73.4 us -> 54.1 us (0.74)
  Pallas kernels: 69.8 us -> 50.6 us
    pallas_call x1, Pallas kernels: 69.8 us -> 50.6 us  [body(): pl.pallas_call(functools.partial(kernel, ndp, nv), out_shape=(jax.ShapeDt...]
where the time goes in v1:
time: 54.1 us; the launch traced here: 53.9 us
  Pallas kernels  50.6 us (94%)
  local copies, waits for them, and re-layouts  2.74 us (5%)
  between operations  0.64 us (1%)
    pallas_call x1, Pallas kernels, body(): pl.pallas_call(functools.partial(kernel, ndp, nv), out_shape=(jax.ShapeDt...  50.6 us
    unnamed x2, local copies, waits for them, and re-layouts  2.74 us

profile of v1, /device:TPU:0, one launch (start us, length us, event | category | flops | bytes accessed | tf_op | source)
XLA Modules:
  0.0 53.9 jit_solution(14426232369973548202)
XLA Ops:
  0.6 50.6 %shard_map.68 = (f32[1,64]{1,0:T(1,128)}, f32[64,448]{1,0:T(8,128)}) custom-call(bf16[64,3584]{1,0:T(8,128)(2,1)} %hid.1, bf16[4752,3584]{1,0:T(8,128)(2,1)} %bitcast.3, s32[64,64]{1,0:T(8,128)} %ids_in.1, f32[64,64]{1,0:T(8,128)} %probs_in.1, f32[1,64]{1,0:T(1,128)} %bitcast.4), custom_call_target="tpu_custom_call" | custom-call | tf_op jit(solution)/shard_map/pallas_call | solution.py:510
  51.2 1.2 %copy.9 = f32[64]{0:T(128)} copy(f32[64]{0:T(128)} %bitcast.5) | data formatting | bytes 512
  52.4 1.6 %copy.10 = f32[64,448]{1,0:T(8,128)} copy(f32[64,448]{1,0:T(8,128)} %get-tuple-element.9) | data formatting | bytes 229376

commit v2 on v1

--- a/solution.py
+++ b/solution.py
@@ -41,7 +41,7 @@
     wv, h_all, ids_v, probs_v, tw_v, tp_all, sp, lt, logits, lg, g, r1, sx, rx, s2, r2, sb, rb, rz,
     stats, picks, cols, cols2, back, own,
     w_sem, l_sem, i_sem, pk_s, pk_r, hx_s, hx_r, hc_s, hc_r, tp_s, tp_r, st_s, st_r,
-    g1_s, g1_r, gx_s, gx_r, g2_s, g2_r, gb_s, gb_r, rz_s, rz_r,
+    g1_s, g1_r, gx_s, gx_r, g2_s, g2_r, gb_s, gb_r, rz_s, rz_r, known,
 ):
     d, mv = lax.axis_index("dp"), lax.axis_index("vocab")
     x, core = d // 2, d % 2
@@ -60,8 +60,9 @@
     runs = runs_of(depth, feat)
     direct = [i >= ng - 4 for i in range(ng)]
     shift = sorted(range(nblk), key=lambda o: (-min(o, nblk - o), o))
-    passed = nblk == 4 and parts[ng - 4][0] <= 2 * group
-    early = [run for run in runs if not direct[run[0]] and not (passed and run[1] == 0)]
+    span = parts[0][1]
+    passed = nblk == 4 and span <= group and parts[ng - 4][0] <= 2 * group
+    early = [run for run in runs if not direct[run[0]] and not (passed and run[0] == 0)]
     late = [run for run in runs if direct[run[0]]]
     mg, mm = mv // q, lax.rem(mv, q)
     other = (2 * x + 1 - core, mv)
@@ -161,10 +162,8 @@
             device_id=(d, pair_of(b) * q + m), device_id_type=MESH)
 
     def rz_copy(i):
-        first, width = parts[i]
-        width = min(width, group - first)
-        return pltpu.make_async_remote_copy(
-            src_ref=s2.at[i, :, 0:width], dst_ref=rz.at[:, first:first + width],
+        return pltpu.make_async_remote_copy(
+            src_ref=s2.at[i, :, 0:span], dst_ref=rz,
             send_sem=rz_s.at[0], recv_sem=rz_r.at[0],
             device_id=(d, lax.rem(mg + nblk - 1, nblk) * q + mm), device_id_type=MESH)
 
@@ -181,14 +180,21 @@
         small_in(i).start()
 
     barrier = pltpu.get_barrier_semaphore()
-
-    def greet(j, _):
-        to = lax.rem(me + j, nd)
-        pl.semaphore_signal(
-            barrier, inc=1, device_id=(to // nv, lax.rem(to, nv)), device_id_type=MESH)
-        return 0
-
-    lax.fori_loop(1, nd, greet, 0)
+    near = [(lax.rem(d + j, ndp), mv) for j in range(1, ndp)]
+    near += [(d, mg * q + lax.rem(mm + j, q)) for j in range(1, q)]
+    near += [(d, lax.rem(mg + j, nblk) * q + mm) for j in sorted({1, nblk - 1} - {0, nblk})]
+    rounds = 1 + (q > 1) + nblk // 2
+
+    def tell(sem):
+        for to in near:
+            pl.semaphore_signal(sem, inc=1, device_id=to, device_id_type=MESH)
+
+    def heard(k):
+        pl.semaphore_wait(known.at[k], len(near))
+        if k + 2 < rounds:
+            tell(known.at[k + 1])
+
+    tell(barrier)
     for lo, hi in pieces:
         w_piece(lo, hi).start()
 
@@ -198,7 +204,7 @@
     tp_all[block(d), 0:top_n] = ids_v[...].astype(jnp.float32)
     tp_all[block(d), top_n:2 * top_n] = probs_v[...]
     drain(h_all.at[block(d), :], l_sem.at[0])
-    pl.semaphore_wait(barrier, nd - 1)
+    pl.semaphore_wait(barrier, len(near))
 
     for j in range(1, nx):
         hx_copy(j, 0).start()
@@ -212,6 +218,8 @@
         for side in range(2):
             tp_copy(2 * lax.rem(x + j, nx) + side, False).start()
 
+    if rounds > 1:
+        tell(known.at[0])
     offset = (me * cols_n).astype(jnp.float32)
     nh = (cols_n + 255) // 256
     lane8 = lax.broadcasted_iota(jnp.int32, (8, 128), 1)
@@ -274,6 +282,8 @@
     top = jnp.full((8, tok), -3e38, jnp.float32)
     turned_tiles = 0
     for c in range(nk):
+        if c >= 4 and c % 2 == 0 and (c - 4) // 2 < rounds - 1:
+            heard((c - 4) // 2)
         if c + 1 < nk:
             forward_in(c + 1)
         drain(h_all.at[0:nx * rows, kpart(c)], hc_r.at[c])
@@ -308,6 +318,8 @@
     total = lax.fori_loop(0, nt * 128 // deep, expsum, jnp.zeros((8, tok), jnp.float32))
     s = jnp.sum(total, axis=0, keepdims=True)
 
+    for k in range(len([c for c in range(4, nk) if c % 2 == 0]), rounds - 1):
+        heard(k)
     for j in range(nb):
         stats[me, j:j + 1, :] = m[:, j * 128:(j + 1) * 128]
         stats[me, nb + j:nb + j + 1, :] = s[:, j * 128:(j + 1) * 128]
@@ -346,6 +358,9 @@
 
     lax.fori_loop(0, tok // 16, grad, 0, unroll=2)
 
+    def waits(run):
+        return passed and run[1] == 2 and parts[run[0]][0] + run[3] < 2 * group + span
+
     def pair_sum(i, jx):
         mine_rows, width = block(2 * lax.rem(x + jx, nx) + core), parts[i][1]
         return g[i, mine_rows, 0:width] + r1[i, jx, :, 0:width]
@@ -359,7 +374,7 @@
                 sb[i, jx, :, 0:width] = both.astype(jnp.bfloat16)
                 for run in late:
                     _, b, m, at, to, wide = run
-                    if run[0] != i or (jx == 0 and passed and b == 2):
+                    if run[0] != i or (jx == 0 and waits(run)):
                         continue
                     if jx == 0 and b == nblk - 1:
                         @pl.when(m == mm)
@@ -383,7 +398,7 @@
         for jx in range(1, nx):
             both += rx[i, jx - 1, :, 0:width].astype(jnp.float32)
         s2[i, :, 0:width] = both.astype(jnp.bfloat16)
-        if passed and parts[i][0] < group:
+        if passed and i == 0:
             rz_copy(i).start()
         for run in early:
             _, b, m, at, to, wide = run
@@ -405,17 +420,16 @@
             lg[...], wv[:, first:first + width], preferred_element_type=jnp.float32)
         for jx in range(nx):
             g1_copy(i, jx).start()
-        if i >= 1:
-            to_x(i - 1)
-        if i >= lag:
-            to_vocab(i - lag)
-        if i == 2 or (ng < 3 and i == ng - 1):
+        if i == 0:
             turned = jnp.sum(cols[...].T, axis=0, keepdims=True)
             for j in range(nb):
                 picks[me, j:j + 1, :] = turned[:, j * 128:(j + 1) * 128]
             for j in range(1, nd):
                 pk_copy(j, me).start()
-
+        if i >= 1:
+            to_x(i - 1)
+        if i >= lag:
+            to_vocab(i - lag)
     to_x(ng - 1)
     for i in range(max(ng - lag, 0), ng):
         to_vocab(i)
@@ -424,15 +438,15 @@
         drain(rz, rz_r.at[0])
         for i in range(ng):
             first, width = parts[i]
-            lo, hi = max(first, 2 * group) - first, min(first + width, 3 * group) - first
-            if lo >= hi:
-                continue
-            mine_rows, at = block(2 * x + core), first + lo - 2 * group
-            sb[i, 0, :, lo:hi] = (
-                g[i, mine_rows, lo:hi] + r1[i, 0, :, lo:hi]
-                + rz[:, at:at + hi - lo].astype(jnp.float32)).astype(jnp.bfloat16)
+            lo, hi = max(first, 2 * group), min(first + width, 2 * group + span)
+            if lo < hi:
+                mine_rows, at = block(2 * x + core), lo - 2 * group
+                lo, hi = lo - first, hi - first
+                sb[i, 0, :, lo:hi] = (
+                    g[i, mine_rows, lo:hi] + r1[i, 0, :, lo:hi]
+                    + rz[:, at:at + hi - lo].astype(jnp.float32)).astype(jnp.bfloat16)
             for run in late:
-                if run[0] == i and run[1] == 2:
+                if run[0] == i and waits(run):
                     gb_copy(run, 0).start()
 
     drain(picks.at[0:nd - 1, 0:nb], pk_r.at[0])
@@ -510,7 +524,7 @@
     div, out = pl.pallas_call(
         functools.partial(kernel, ndp, nv),
         out_shape=(
-            jax.ShapeDtypeStruct((1, rows), f32), jax.ShapeDtypeStruct((rows, feat), f32)),
+            pltpu.VMEM((1, rows), f32), pltpu.VMEM((rows, feat), f32)),
         in_specs=[anyspace] * 5,
         out_specs=(vmem, vmem),
         scratch_shapes=[
@@ -524,7 +538,7 @@
             pltpu.VMEM((ng, nx - 1, rows, gw), bf16),
             pltpu.VMEM((ng, nx - 1, rows, gw), bf16),
             pltpu.VMEM((ng, rows, gw), bf16), pltpu.VMEM((nv, rows, ww), bf16),
-            pltpu.VMEM((ng, nx, rows, gw), bf16), pltpu.VMEM((nx * nv, rows, ww), bf16), pltpu.VMEM((rows, q * feat), bf16),
+            pltpu.VMEM((ng, nx, rows, gw), bf16), pltpu.VMEM((nx * nv, rows, ww), bf16), pltpu.VMEM((rows, gw), bf16),
             pltpu.VMEM((nd, srows, 128), f32), pltpu.VMEM((nd, prows, 128), f32),
             pltpu.VMEM((tok, 128), f32), pltpu.VMEM((tok, 128), f32),
             pltpu.VMEM((128, tok), f32), pltpu.VMEM((rows, ww), f32),
@@ -532,9 +546,10 @@
             dma((1,)), dma((nk,)), dma((1,)), dma((nk,)), dma((1,)), dma((2,)),
             dma((1,)), dma((1,)), dma((1,)), dma((ng,)), dma((1,)), dma((ng,)),
             dma((1,)), dma((1,)), dma((1,)), dma((1,)), dma((1,)), dma((1,)),
+            pltpu.SemaphoreType.REGULAR((8,)),
         ],
         compiler_params=pltpu.CompilerParams(
-            collective_id=0, has_side_effects=True, vmem_limit_bytes=67043328),
+            collective_id=0, has_side_effects=True, vmem_limit_bytes=66600000),
     )(hidden, head_weight.T, teacher_ids, teacher_probs, token_weight[None, :])
     return div[0], out
 

time: 54.1 us -> 51.2 us (0.946)
  local copies, waits for them, and re-layouts: 2.74 us -> 1.17 us
  Pallas kernels: 50.6 us -> 49.2 us
    unnamed x2, local copies, waits for them, and re-layouts: 2.74 us -> 1.17 us
    pallas_call x1, Pallas kernels: 50.6 us -> 49.2 us  [body(): pl.pallas_call(functools.partial(kernel, ndp, nv), out_shape=(pltpu.VMEM(...]
where the time goes in v2:
time: 51.2 us; the launch traced here: 51 us
  Pallas kernels  49.2 us (96%)
  local copies, waits for them, and re-layouts  1.17 us (2%)
  between operations  0.64 us (1%)
    pallas_call x1, Pallas kernels, body(): pl.pallas_call(functools.partial(kernel, ndp, nv), out_shape=(pltpu.VMEM(...  49.2 us
    unnamed x2, local copies, waits for them, and re-layouts  1.17 us

profile of v2, /device:TPU:0, one launch (start us, length us, event | category | flops | bytes accessed | tf_op | source)
XLA Modules:
  0.0 51.0 jit_solution(9210053873642625366)
XLA Ops:
  0.6 49.2 %shard_map.68 = (f32[1,64]{1,0:T(1,128)S(1)}, f32[64,448]{1,0:T(8,128)S(1)}) custom-call(bf16[64,3584]{1,0:T(8,128)(2,1)} %hid.1, bf16[4752,3584]{1,0:T(8,128)(2,1)} %bitcast.4, s32[64,64]{1,0:T(8,128)} %ids_in.1, f32[64,64]{1,0:T(8,128)} %probs_in.1, f32[1,64]{1,0:T(1,128)} %bitcast.5), custom_call_target="tpu_custom_call" | custom-call | tf_op jit(solution)/shard_map/pallas_call | solution.py:524
  49.8 0.5 %copy.9 = f32[64]{0:T(128)} copy(f32[64]{0:T(128)S(1)} %bitcast.3) | data formatting | bytes 512
  50.4 0.7 %copy.10 = f32[64,448]{1,0:T(8,128)} copy(f32[64,448]{1,0:T(8,128)S(1)} %get-tuple-element.7) | data formatting | bytes 229376

commit v3 on v2

--- a/solution.py
+++ b/solution.py
@@ -58,10 +58,11 @@
     q, ww, starts = windows(feat)
     nblk, group = nv // q, q * feat
     runs = runs_of(depth, feat)
-    direct = [i >= ng - 4 for i in range(ng)]
+    direct = [i >= ng - 2 for i in range(ng)]
     shift = sorted(range(nblk), key=lambda o: (-min(o, nblk - o), o))
     span = parts[0][1]
-    passed = nblk == 4 and span <= group and parts[ng - 4][0] <= 2 * group
+    passed = nblk == 4 and span <= group and 3 * span <= 2 * group and (
+        parts[ng - 2][0] >= 2 * group + span)
     early = [run for run in runs if not direct[run[0]] and not (passed and run[0] == 0)]
     late = [run for run in runs if direct[run[0]]]
     mg, mm = mv // q, lax.rem(mv, q)
@@ -358,9 +359,6 @@
 
     lax.fori_loop(0, tok // 16, grad, 0, unroll=2)
 
-    def waits(run):
-        return passed and run[1] == 2 and parts[run[0]][0] + run[3] < 2 * group + span
-
     def pair_sum(i, jx):
         mine_rows, width = block(2 * lax.rem(x + jx, nx) + core), parts[i][1]
         return g[i, mine_rows, 0:width] + r1[i, jx, :, 0:width]
@@ -374,7 +372,7 @@
                 sb[i, jx, :, 0:width] = both.astype(jnp.bfloat16)
                 for run in late:
                     _, b, m, at, to, wide = run
-                    if run[0] != i or (jx == 0 and waits(run)):
+                    if run[0] != i:
                         continue
                     if jx == 0 and b == nblk - 1:
                         @pl.when(m == mm)
@@ -392,11 +390,18 @@
     def to_vocab(i):
         if direct[i]:
             return
-        width = parts[i][1]
+        first, width = parts[i]
         both = pair_sum(i, 0)
         drain(rx.at[i, :, :, 0:width], gx_r.at[i])
         for jx in range(1, nx):
             both += rx[i, jx - 1, :, 0:width].astype(jnp.float32)
+        if passed:
+            lo, hi = max(first, 2 * group), min(first + width, 2 * group + span)
+            if lo < hi:
+                added = rz[:, lo - 2 * group:hi - 2 * group].astype(jnp.float32)
+                pad = [jnp.zeros((rows, n), jnp.float32) for n in (lo - first, first + width - hi)]
+                both += jnp.concatenate(
+                    [p for p in (pad[0], added, pad[1]) if p.shape[1] > 0], axis=1)
         s2[i, :, 0:width] = both.astype(jnp.bfloat16)
         if passed and i == 0:
             rz_copy(i).start()
@@ -413,41 +418,30 @@
             else:
                 g2_copy(run).start()
 
-    lag = 3
+    lag, head = 3, 3 if passed else ng
     for i in range(ng):
         first, width = parts[i]
         g[i, :, 0:width] = jnp.dot(
             lg[...], wv[:, first:first + width], preferred_element_type=jnp.float32)
         for jx in range(nx):
             g1_copy(i, jx).start()
-        if i == 0:
+        if i >= 1:
+            to_x(i - 1)
+        if i == min(1, ng - 1):
             turned = jnp.sum(cols[...].T, axis=0, keepdims=True)
             for j in range(nb):
                 picks[me, j:j + 1, :] = turned[:, j * 128:(j + 1) * 128]
             for j in range(1, nd):
                 pk_copy(j, me).start()
-        if i >= 1:
-            to_x(i - 1)
-        if i >= lag:
+        if lag <= i < lag + head:
             to_vocab(i - lag)
-    to_x(ng - 1)
-    for i in range(max(ng - lag, 0), ng):
-        to_vocab(i)
-
+    rest = list(range(max(min(head, ng - lag), 0), ng))
     if passed:
         drain(rz, rz_r.at[0])
-        for i in range(ng):
-            first, width = parts[i]
-            lo, hi = max(first, 2 * group), min(first + width, 2 * group + span)
-            if lo < hi:
-                mine_rows, at = block(2 * x + core), lo - 2 * group
-                lo, hi = lo - first, hi - first
-                sb[i, 0, :, lo:hi] = (
-                    g[i, mine_rows, lo:hi] + r1[i, 0, :, lo:hi]
-                    + rz[:, at:at + hi - lo].astype(jnp.float32)).astype(jnp.bfloat16)
-            for run in late:
-                if run[0] == i and waits(run):
-                    gb_copy(run, 0).start()
+        to_vocab(rest.pop(0))
+    to_x(ng - 1)
+    for i in rest:
+        to_vocab(i)
 
     drain(picks.at[0:nd - 1, 0:nb], pk_r.at[0])
     for j in range(nb):

time: 51.2 us -> 49.9 us (0.975)
  Pallas kernels: 49.2 us -> 47.9 us
    pallas_call x1, Pallas kernels: 49.2 us -> 47.9 us  [body(): pl.pallas_call(functools.partial(kernel, ndp, nv), out_shape=(pltpu.VMEM(...]
where the time goes in v3:
time: 49.9 us; the launch traced here: 49.7 us
  Pallas kernels  47.9 us (96%)
  local copies, waits for them, and re-layouts  1.17 us (2%)
  between operations  0.64 us (1%)
    pallas_call x1, Pallas kernels, body(): pl.pallas_call(functools.partial(kernel, ndp, nv), out_shape=(pltpu.VMEM(...  47.9 us
    unnamed x2, local copies, waits for them, and re-layouts  1.17 us

profile of v3, /device:TPU:0, one launch (start us, length us, event | category | flops | bytes accessed | tf_op | source)
XLA Modules:
  0.0 49.7 jit_solution(4297593203503844232)
XLA Ops:
  0.6 47.9 %shard_map.68 = (f32[1,64]{1,0:T(1,128)S(1)}, f32[64,448]{1,0:T(8,128)S(1)}) custom-call(bf16[64,3584]{1,0:T(8,128)(2,1)} %hid.1, bf16[4752,3584]{1,0:T(8,128)(2,1)} %bitcast.4, s32[64,64]{1,0:T(8,128)} %ids_in.1, f32[64,64]{1,0:T(8,128)} %probs_in.1, f32[1,64]{1,0:T(1,128)} %bitcast.5), custom_call_target="tpu_custom_call" | custom-call | tf_op jit(solution)/shard_map/pallas_call | solution.py:518
  48.5 0.5 %copy.9 = f32[64]{0:T(128)} copy(f32[64]{0:T(128)S(1)} %bitcast.3) | data formatting | bytes 512
  49.0 0.7 %copy.10 = f32[64,448]{1,0:T(8,128)} copy(f32[64,448]{1,0:T(8,128)S(1)} %get-tuple-element.7) | data formatting | bytes 229376
